TPU v7x, 256 devices: a whole 4x4x8 slice. The times are simulated.
256 devices in a mesh: seq: 16 (over x, y_lo, core), exp: 16 (over y_hi, z).
Axes of the slice: x: 4, y: 4 (y_hi: 2, y_lo: 2; y = y_hi * 2 + y_lo), z: 8, core: 2. Of those that a mesh axis runs over, the one named last changes fastest.
Arguments:
- queries: bfloat16 [8, 4096, 2048], P(None, 'seq', 'exp'), may hold values from -5 to 5
- keys: bfloat16 [8, 4096, 2048], P(None, 'seq', 'exp'), may hold values from -5 to 5
- values: bfloat16 [8, 4096, 2048], P(None, 'seq', 'exp'), may hold values from -170 to 170
- seg_ids: int32 [8, 4096], replicated, may hold values from 0 to 3, as said below
- norm_gain: float32 [2048], replicated, may hold values from 0.25 to 1.75
- router_w: bfloat16 [512, 64], replicated, may hold values from -0.25 to 0.25
- expert_ids: int32 [4096, 8, 4, 2], P(('seq', 'exp')), may hold values from 0 to 63, all different within a row; in each aligned block of 512 rows (0 to 511, 512 to 1023, ..., all dimensions but the last counted through in order) at most 32 rows name the same one
- w_in: bfloat16 [64, 512, 1024], P('exp'), may hold values from -0.25 to 0.25
- w_out: bfloat16 [64, 1024, 512], P('exp'), may hold values from -0.1875 to 0.1875
Outputs:
- normed: bfloat16 [8, 4096, 2048], P(None, ('seq', 'exp'))
- expert_mix: bfloat16 [8, 4096, 2048], P(None, ('seq', 'exp'))
Inputs may be any that keep to these rules, and one draw needn't show every extreme that they name: `seg_ids`: in each sequence the numbers start at 0, never fall, and rise by one at each of 3 document starts; every start lies at an even position after the middle of the sequence. `expert_ids`: the 2 experts of a sub-token differ. Among the rows of one device (its 16 positions, all sequences, all sub-tokens) no expert is named more than 32 times; in every draw some device names some expert exactly 32 times.
All inputs are finite; a program needn't handle non-finite values.
Results may differ from a plain program's by a relative error of at most 0.015.
Values may be sent and summed in bfloat16 or wider, within the bound.
A program may use at most 128 MiB of HBM per device.

v0:
```python
import jax
import jax.numpy as jnp
from jax import lax
from jax.sharding import PartitionSpec as P

HD = 128
SUB = 512
TOPK = 2
CAP = 32
NEG = -1e30


def update(running, query_heads, shaped, query_pos, query_seg, key_pos, key_seg, score_scale):
    maxima, totals, running_total = running
    attention_scores = (
        jnp.einsum("bqhd,bkhd->bhqk", query_heads, shaped[0], preferred_element_type=jnp.float32)
        * score_scale
    )
    visible = (key_pos[None, :] <= query_pos[:, None])[None, None] & (
        key_seg[:, None, None, :] == query_seg[:, None, :, None]
    )
    highest = jnp.max(jnp.where(visible, attention_scores, NEG), axis=-1)
    new_max = jnp.maximum(maxima, highest)
    weights = jnp.where(visible, jnp.exp(attention_scores - new_max[..., None]), 0.0)
    rescale_factor = jnp.exp(maxima - new_max)
    totals = totals * rescale_factor + jnp.sum(weights, axis=-1)
    rounded_result = weights.astype(jnp.bfloat16)
    running_total = running_total * rescale_factor[..., None] + jnp.einsum(
        "bhqk,bkhd->bhqd", rounded_result, shaped[1], preferred_element_type=jnp.float32
    )
    return (new_max, totals, running_total)


def attend_block(
    running, query_heads, block, query_pos, query_seg, seg_ids, key_first, score_scale
):
    row_count = block.shape[2]
    key_pos = key_first + jnp.arange(row_count, dtype=jnp.int32)
    key_seg = lax.dynamic_slice_in_dim(seg_ids, key_first, row_count, 1)
    needed = (key_first <= query_pos[-1]) & jnp.any(key_seg[:, -1] >= query_seg[:, 0])
    shaped = block.reshape(2, block.shape[1], row_count, query_heads.shape[2], query_heads.shape[3])
    return lax.cond(
        needed,
        lambda state: update(
            state, query_heads, shaped, query_pos, query_seg, key_pos, key_seg, score_scale
        ),
        lambda state: state,
        running,
    )


def body(queries, keys, values, seg_ids, norm_gain, router_w, expert_ids, w_in, w_out):
    my_index = lax.axis_index("seq")
    seq_count, local_len, local_width = queries.shape
    head_count = local_width // HD
    score_scale = HD ** (-0.5)
    first_pos = my_index * local_len
    query_pos = first_pos + jnp.arange(local_len, dtype=jnp.int32)
    query_seg = lax.dynamic_slice_in_dim(seg_ids, first_pos, local_len, 1)
    query_heads = queries.reshape(seq_count, local_len, head_count, HD)
    initial = (
        jnp.full((seq_count, head_count, local_len), NEG, jnp.float32),
        jnp.zeros((seq_count, head_count, local_len), jnp.float32),
        jnp.zeros((seq_count, head_count, local_len, HD), jnp.float32),
    )
    stacked = jnp.stack([keys, values])

    def attend(running, block, key_first):
        return attend_block(
            running, query_heads, block, query_pos, query_seg, seg_ids, key_first, score_scale
        )

    shard_part = lax.all_gather(stacked, "seq", axis=2, tiled=True)
    row_count = shard_part.shape[2]
    width = min(row_count, local_len)
    repeats = row_count // width

    def inner(number, state):
        section = lax.dynamic_slice_in_dim(shard_part, number * width, width, 2)
        return attend(state, section, number * width)

    running = lax.fori_loop(0, repeats, inner, initial)
    maxima, totals, running_total = running
    attended = (
        (running_total / totals[..., None])
        .transpose(0, 2, 1, 3)
        .reshape(seq_count, local_len, local_width)
        .astype(jnp.bfloat16)
    )
    tokens = lax.all_to_all(attended, "exp", split_axis=1, concat_axis=2, tiled=True)
    values32 = tokens.astype(jnp.float32)
    spread = jnp.sqrt(jnp.mean(values32 * values32, axis=-1, keepdims=True) + 1e-06)
    normed = (values32 / spread * norm_gain).astype(jnp.bfloat16)
    token_count = normed.shape[1]
    feature_count = normed.shape[2]
    sub_count = feature_count // SUB
    sub_rows = (
        normed.reshape(seq_count, token_count, sub_count, SUB)
        .transpose(1, 0, 2, 3)
        .reshape(-1, SUB)
    )
    picks = expert_ids.reshape(-1, TOPK)
    logits = jnp.dot(sub_rows, router_w, preferred_element_type=jnp.float32)
    chosen = jnp.take_along_axis(logits, picks, axis=1)
    sigmas = jax.nn.sigmoid(chosen)
    gates = sigmas / jnp.sum(sigmas, axis=1, keepdims=True)
    expert_total = router_w.shape[1]
    targets = picks.reshape(-1)
    one_hot = (targets[:, None] == jnp.arange(expert_total, dtype=jnp.int32)[None, :]).astype(
        jnp.int32
    )
    earlier = jnp.cumsum(one_hot, axis=0) - one_hot
    slot_rank = jnp.sum(earlier * one_hot, axis=1)
    destination = targets * CAP + slot_rank
    sources = jnp.arange(targets.shape[0], dtype=jnp.int32) // TOPK
    outgoing = (
        jnp.zeros((expert_total * CAP, SUB), jnp.bfloat16)
        .at[destination]
        .set(sub_rows[sources])
        .reshape(expert_total, CAP, SUB)
    )
    arrived = lax.all_to_all(outgoing, "exp", split_axis=0, concat_axis=1, tiled=True)
    hidden = jax.nn.gelu(
        jnp.einsum("ecs,esf->ecf", arrived, w_in, preferred_element_type=jnp.float32),
        approximate=True,
    ).astype(jnp.bfloat16)
    results = jnp.einsum("ecf,efs->ecs", hidden, w_out, preferred_element_type=jnp.float32).astype(
        jnp.bfloat16
    )
    returned = lax.all_to_all(results, "exp", split_axis=1, concat_axis=0, tiled=True).reshape(
        expert_total * CAP, SUB
    )
    picked = returned[destination].reshape(-1, TOPK, SUB).astype(jnp.float32)
    mixed = jnp.sum(gates[:, :, None] * picked, axis=1).astype(jnp.bfloat16)
    expert_mix = mixed.reshape(token_count, seq_count, feature_count).transpose(1, 0, 2)
    return (normed, expert_mix)


def solution(mesh):
    return jax.shard_map(
        body,
        mesh=mesh,
        in_specs=(
            P(None, "seq", "exp"),
            P(None, "seq", "exp"),
            P(None, "seq", "exp"),
            P(),
            P(),
            P(),
            P(("seq", "exp"), None, None, None),
            P("exp", None, None),
            P("exp", None, None),
        ),
        out_specs=(P(None, ("seq", "exp"), None), P(None, ("seq", "exp"), None)),
        check_vma=False,
    )
```

profile of v0, /device:TPU:7, one launch (start us, length us, event | category | flops | bytes accessed | tf_op | source)
XLA Modules:
  0.0 494.1 jit_solution(5540001684064581826)
XLA Ops:
  7.2 2.3 pad_maximum_fusion
  12.8 94.3 %all-gather.2.cloned.1.call-done = bf16[2,8,4096,128]{3,2,1,0:T(8,128)(2,1)} async-done(((bf16[2,8,256,128]{3,2,1,0:T(8,128)(2,1)}), bf16[2,8,4096,128]{3,2,1,0:T(8,128)(2,1)}) %all-gather.2.cloned.1.call-update) | async-done | bytes 16777232 | tf_op jit(solution)/shard_map/all_gather | solution.py:73
  107.8 198.1 %while.17 = (s32[]{:T(128)}, f32[8,1,256]{2,0,1:T(8,128)S(1)}, f32[8,1,256]{2,0,1:T(8,128)}, f32[8,1,256,128]{3,2,0,1:T(8,128)S(1)}, s32[256]{0:T(256)}, /*index...) while((s32[]{:T(128)}, f32[8,1,256]{2,0,1:T(8,128)S(1)}, ...), condition=%wide.region_6.7_spmd, body=%wide.region_0.6_spmd.sunk | while | flops 277944608 | bytes 10492413 | solution.py:82
  112.4 8.8 %conditional.2 = ((f32[8,1,256]{2,0,1:T(8,128)S(1)}, f32[8,1,256]{2,0,1:T(8,128)}, f32[8,1,256,128]{3,2,0,1:T(8,128)S(1)})) conditional(s32[]{:T(128)} %convert_element_type.119, (f32[8,1,256]{2,0,1:T(8,128)S(1)}, f32[8,1,256]{2,0,1:T(8,128)}, f32[8,1,256,128]{3,2,0,1:T(8,128)S(1)}) %tuple.51, (s32[]{:T(128)}, s32[256]{0:T(256)S(1)}, s32[256]{0:T(256)}, ...), branch_computations={%region_2.0_spmd, %region_3.5_spmd} | conditional | flops 277944576 | bytes 10474604 | solution.py:42
  113.3 2.1 fusion
  115.9 2.4 fusion.5
  118.4 1.5 fusion.4
  125.9 8.8 %conditional.2 = ((f32[8,1,256]{2,0,1:T(8,128)S(1)}, f32[8,1,256]{2,0,1:T(8,128)}, f32[8,1,256,128]{3,2,0,1:T(8,128)S(1)})) conditional(s32[]{:T(128)} %convert_element_type.119, (f32[8,1,256]{2,0,1:T(8,128)S(1)}, f32[8,1,256]{2,0,1:T(8,128)}, f32[8,1,256,128]{3,2,0,1:T(8,128)S(1)}) %tuple.51, (s32[]{:T(128)}, s32[256]{0:T(256)S(1)}, s32[256]{0:T(256)}, ...), branch_computations={%region_2.0_spmd, %region_3.5_spmd} | conditional | flops 277944576 | bytes 10474604 | solution.py:42
  126.7 2.1 fusion
  129.4 2.4 fusion.5
  131.9 1.5 fusion.4
  139.4 8.8 %conditional.2 = ((f32[8,1,256]{2,0,1:T(8,128)S(1)}, f32[8,1,256]{2,0,1:T(8,128)}, f32[8,1,256,128]{3,2,0,1:T(8,128)S(1)})) conditional(s32[]{:T(128)} %convert_element_type.119, (f32[8,1,256]{2,0,1:T(8,128)S(1)}, f32[8,1,256]{2,0,1:T(8,128)}, f32[8,1,256,128]{3,2,0,1:T(8,128)S(1)}) %tuple.51, (s32[]{:T(128)}, s32[256]{0:T(256)S(1)}, s32[256]{0:T(256)}, ...), branch_computations={%region_2.0_spmd, %region_3.5_spmd} | conditional | flops 277944576 | bytes 10474604 | solution.py:42
  140.2 2.1 fusion
  142.9 2.4 fusion.5
  145.3 1.5 fusion.4
  152.9 8.8 %conditional.2 = ((f32[8,1,256]{2,0,1:T(8,128)S(1)}, f32[8,1,256]{2,0,1:T(8,128)}, f32[8,1,256,128]{3,2,0,1:T(8,128)S(1)})) conditional(s32[]{:T(128)} %convert_element_type.119, (f32[8,1,256]{2,0,1:T(8,128)S(1)}, f32[8,1,256]{2,0,1:T(8,128)}, f32[8,1,256,128]{3,2,0,1:T(8,128)S(1)}) %tuple.51, (s32[]{:T(128)}, s32[256]{0:T(256)S(1)}, s32[256]{0:T(256)}, ...), branch_computations={%region_2.0_spmd, %region_3.5_spmd} | conditional | flops 277944576 | bytes 10474604 | solution.py:42
  153.7 2.1 fusion
  156.4 2.4 fusion.5
  158.8 1.5 fusion.4
  166.3 8.8 %conditional.2 = ((f32[8,1,256]{2,0,1:T(8,128)S(1)}, f32[8,1,256]{2,0,1:T(8,128)}, f32[8,1,256,128]{3,2,0,1:T(8,128)S(1)})) conditional(s32[]{:T(128)} %convert_element_type.119, (f32[8,1,256]{2,0,1:T(8,128)S(1)}, f32[8,1,256]{2,0,1:T(8,128)}, f32[8,1,256,128]{3,2,0,1:T(8,128)S(1)}) %tuple.51, (s32[]{:T(128)}, s32[256]{0:T(256)S(1)}, s32[256]{0:T(256)}, ...), branch_computations={%region_2.0_spmd, %region_3.5_spmd} | conditional | flops 277944576 | bytes 10474604 | solution.py:42
  167.2 2.1 fusion
  169.9 2.4 fusion.5
  179.8 8.8 %conditional.2 = ((f32[8,1,256]{2,0,1:T(8,128)S(1)}, f32[8,1,256]{2,0,1:T(8,128)}, f32[8,1,256,128]{3,2,0,1:T(8,128)S(1)})) conditional(s32[]{:T(128)} %convert_element_type.119, (f32[8,1,256]{2,0,1:T(8,128)S(1)}, f32[8,1,256]{2,0,1:T(8,128)}, f32[8,1,256,128]{3,2,0,1:T(8,128)S(1)}) %tuple.51, (s32[]{:T(128)}, s32[256]{0:T(256)S(1)}, s32[256]{0:T(256)}, ...), branch_computations={%region_2.0_spmd, %region_3.5_spmd} | conditional | flops 277944576 | bytes 10474604 | solution.py:42
  180.6 2.1 fusion
  183.3 2.4 fusion.5
  193.3 8.8 %conditional.2 = ((f32[8,1,256]{2,0,1:T(8,128)S(1)}, f32[8,1,256]{2,0,1:T(8,128)}, f32[8,1,256,128]{3,2,0,1:T(8,128)S(1)})) conditional(s32[]{:T(128)} %convert_element_type.119, (f32[8,1,256]{2,0,1:T(8,128)S(1)}, f32[8,1,256]{2,0,1:T(8,128)}, f32[8,1,256,128]{3,2,0,1:T(8,128)S(1)}) %tuple.51, (s32[]{:T(128)}, s32[256]{0:T(256)S(1)}, s32[256]{0:T(256)}, ...), branch_computations={%region_2.0_spmd, %region_3.5_spmd} | conditional | flops 277944576 | bytes 10474604 | solution.py:42
  194.1 2.1 fusion
  196.8 2.4 fusion.5
  206.8 8.8 %conditional.2 = ((f32[8,1,256]{2,0,1:T(8,128)S(1)}, f32[8,1,256]{2,0,1:T(8,128)}, f32[8,1,256,128]{3,2,0,1:T(8,128)S(1)})) conditional(s32[]{:T(128)} %convert_element_type.119, (f32[8,1,256]{2,0,1:T(8,128)S(1)}, f32[8,1,256]{2,0,1:T(8,128)}, f32[8,1,256,128]{3,2,0,1:T(8,128)S(1)}) %tuple.51, (s32[]{:T(128)}, s32[256]{0:T(256)S(1)}, s32[256]{0:T(256)}, ...), branch_computations={%region_2.0_spmd, %region_3.5_spmd} | conditional | flops 277944576 | bytes 10474604 | solution.py:42
  207.6 2.1 fusion
  210.3 2.4 fusion.5
  220.2 8.8 %conditional.2 = ((f32[8,1,256]{2,0,1:T(8,128)S(1)}, f32[8,1,256]{2,0,1:T(8,128)}, f32[8,1,256,128]{3,2,0,1:T(8,128)S(1)})) conditional(s32[]{:T(128)} %convert_element_type.119, (f32[8,1,256]{2,0,1:T(8,128)S(1)}, f32[8,1,256]{2,0,1:T(8,128)}, f32[8,1,256,128]{3,2,0,1:T(8,128)S(1)}) %tuple.51, (s32[]{:T(128)}, s32[256]{0:T(256)S(1)}, s32[256]{0:T(256)}, ...), branch_computations={%region_2.0_spmd, %region_3.5_spmd} | conditional | flops 277944576 | bytes 10474604 | solution.py:42
  221.1 2.1 fusion
  223.8 2.4 fusion.5
  233.7 8.8 %conditional.2 = ((f32[8,1,256]{2,0,1:T(8,128)S(1)}, f32[8,1,256]{2,0,1:T(8,128)}, f32[8,1,256,128]{3,2,0,1:T(8,128)S(1)})) conditional(s32[]{:T(128)} %convert_element_type.119, (f32[8,1,256]{2,0,1:T(8,128)S(1)}, f32[8,1,256]{2,0,1:T(8,128)}, f32[8,1,256,128]{3,2,0,1:T(8,128)S(1)}) %tuple.51, (s32[]{:T(128)}, s32[256]{0:T(256)S(1)}, s32[256]{0:T(256)}, ...), branch_computations={%region_2.0_spmd, %region_3.5_spmd} | conditional | flops 277944576 | bytes 10474604 | solution.py:42
  234.6 2.1 fusion
  237.2 2.4 fusion.5
  247.2 8.8 %conditional.2 = ((f32[8,1,256]{2,0,1:T(8,128)S(1)}, f32[8,1,256]{2,0,1:T(8,128)}, f32[8,1,256,128]{3,2,0,1:T(8,128)S(1)})) conditional(s32[]{:T(128)} %convert_element_type.119, (f32[8,1,256]{2,0,1:T(8,128)S(1)}, f32[8,1,256]{2,0,1:T(8,128)}, f32[8,1,256,128]{3,2,0,1:T(8,128)S(1)}) %tuple.51, (s32[]{:T(128)}, s32[256]{0:T(256)S(1)}, s32[256]{0:T(256)}, ...), branch_computations={%region_2.0_spmd, %region_3.5_spmd} | conditional | flops 277944576 | bytes 10474604 | solution.py:42
  248.0 2.1 fusion
  250.7 2.4 fusion.5
  260.7 8.8 %conditional.2 = ((f32[8,1,256]{2,0,1:T(8,128)S(1)}, f32[8,1,256]{2,0,1:T(8,128)}, f32[8,1,256,128]{3,2,0,1:T(8,128)S(1)})) conditional(s32[]{:T(128)} %convert_element_type.119, (f32[8,1,256]{2,0,1:T(8,128)S(1)}, f32[8,1,256]{2,0,1:T(8,128)}, f32[8,1,256,128]{3,2,0,1:T(8,128)S(1)}) %tuple.51, (s32[]{:T(128)}, s32[256]{0:T(256)S(1)}, s32[256]{0:T(256)}, ...), branch_computations={%region_2.0_spmd, %region_3.5_spmd} | conditional | flops 277944576 | bytes 10474604 | solution.py:42
  261.5 2.1 fusion
  264.2 2.4 fusion.5
  274.2 8.8 %conditional.2 = ((f32[8,1,256]{2,0,1:T(8,128)S(1)}, f32[8,1,256]{2,0,1:T(8,128)}, f32[8,1,256,128]{3,2,0,1:T(8,128)S(1)})) conditional(s32[]{:T(128)} %convert_element_type.119, (f32[8,1,256]{2,0,1:T(8,128)S(1)}, f32[8,1,256]{2,0,1:T(8,128)}, f32[8,1,256,128]{3,2,0,1:T(8,128)S(1)}) %tuple.51, (s32[]{:T(128)}, s32[256]{0:T(256)S(1)}, s32[256]{0:T(256)}, ...), branch_computations={%region_2.0_spmd, %region_3.5_spmd} | conditional | flops 277944576 | bytes 10474604 | solution.py:42
  275.0 2.1 fusion
  277.7 2.4 fusion.5
  287.6 8.8 %conditional.2 = ((f32[8,1,256]{2,0,1:T(8,128)S(1)}, f32[8,1,256]{2,0,1:T(8,128)}, f32[8,1,256,128]{3,2,0,1:T(8,128)S(1)})) conditional(s32[]{:T(128)} %convert_element_type.119, (f32[8,1,256]{2,0,1:T(8,128)S(1)}, f32[8,1,256]{2,0,1:T(8,128)}, f32[8,1,256,128]{3,2,0,1:T(8,128)S(1)}) %tuple.51, (s32[]{:T(128)}, s32[256]{0:T(256)S(1)}, s32[256]{0:T(256)}, ...), branch_computations={%region_2.0_spmd, %region_3.5_spmd} | conditional | flops 277944576 | bytes 10474604 | solution.py:42
  288.5 2.1 fusion
  291.2 2.4 fusion.5
  308.3 9.0 %all-to-all-start = ((bf16[8,256,128]{2,0,1:T(8,128)(2,1)}), bf16[8,256,128]{2,0,1:T(8,128)(2,1)S(1)}, u32[]{:S(2)}, u32[]{:S(2)}) async-start(bf16[8,256,128]{2,0,1:T(8,128)(2,1)} %fusion.38), calls=%async_computation | async-start | bytes 1048576 | tf_op jit(solution)/shard_map/all_to_all | solution.py:90
  317.6 18.0 %reduce-window.6 = s32[64,8,128]{2,1,0:T(8,128)S(1)} reduce-window(s32[64,8,128]{2,1,0:T(8,128)S(1)} %copy-done.2, s32[]{:T(128)} %constant.101.clone.1), window={size=1x1x128 pad=0_0x0_0x127_0}, to_apply=%region_10.11 | reduce-window | flops 8323072 | bytes 524292 | tf_op jit(solution)/shard_map/reduce-window
  337.0 1.6 copy.143
  338.6 1.6 reshape.311
  341.8 13.1 %scatter_custom_fusion = bf16[2048,512]{1,0:T(8,128)(2,1)S(1)} fusion(s32[1024]{0:T(1024)S(1)} %bitcast.122, bf16[512,512]{1,0:T(8,128)(2,1)} %reshape.305, s32[1024]{0:T(1024)S(1)} %broadcast_clamp_fusion.1, bf16[]{:T(256)} %constant.114.clone.1), kind=kCustom, calls=%fused_computation.52 | custom fusion | bytes 2097664 | tf_op jit(solution)/shard_map/scatter | solution.py:119
  354.9 52.7 %all_to_all.42 = bf16[64,32,512]{2,1,0:T(8,128)(2,1)S(1)} all-to-all(bf16[64,32,512]{2,1,0:T(8,128)(2,1)S(1)} %bitcast.110), channel_id=1, replica_groups=mesh['seq'=16,'exp'=16] {'exp'}, dimensions={0} | all-to-all | bytes 4194304 | tf_op jit(solution)/shard_map/all_to_all | solution.py:122
  407.9 9.7 %fusion.31 = bf16[4,512,512]{2,1,0:T(8,128)(2,1)} fusion(bf16[4,1024,512]{2,1,0:T(8,128)(2,1)} %param.21, bf16[4,512,512]{2,1,0:T(8,128)(2,1)S(1)} %bitcast.114, bf16[4,512,1024]{2,1,0:T(8,128)(2,1)} %param.20), kind=kOutput, calls=%fused_computation.48 | convolution fusion | flops 4314890240 | bytes 12582912 | tf_op jit(solution)/shard_map/ecf,efs->ecs/dot_general | solution.py:127
  417.6 4.6 copy.159
  422.2 4.5 all-to-all-start.2
  428.8 8.6 %gather_fusion.1 = f32[1024]{0:T(1024)S(1)} fusion(f32[512,64]{0,1:T(8,128)S(1)} %fusion.54, s32[1024]{0:T(1024)S(1)} %reshape.331), kind=kCustom, calls=%fused_computation.2 | custom fusion | bytes 16384 | tf_op jit(solution)/shard_map/jit(take_along_axis)/gather | solution.py:104
  438.7 1.6 copy.140
  444.5 29.3 %all-to-all-done.2 = bf16[4,512,512]{2,0,1:T(4,128)(2,1)S(1)} async-done(((bf16[4,512,512]{2,0,1:T(4,128)(2,1)}), bf16[4,512,512]{2,0,1:T(4,128)(2,1)S(1)}, u32[]{:S(2)}, u32[]{:S(2)}) %all-to-all-start.2) | async-done | bytes 2097184 | tf_op jit(solution)/shard_map/all_to_all | solution.py:130
  475.1 2.2 copy.160
  477.3 4.0 gather_fusion
  482.6 3.2 multiply_reduce_fusion
  (274 shorter events, 129.2 us)
Async XLA Ops:
  7.2 420.3 %copy-start = (bf16[512,64]{0,1:T(8,128)(2,1)S(1)}, bf16[512,64]{0,1:T(8,128)(2,1)}, u32[]{:S(2)}) copy-start(bf16[512,64]{0,1:T(8,128)(2,1)} %param.18) | copy-start | bytes 196612
  7.2 2.4 copy-start.5
  7.2 99.9 %all-gather.2.cloned.1.call-start = ((), (), s32[]{:S(2)}) async-start(), calls=%async_computation.3 | async-start | bytes 17825792 | tf_op jit(solution)/shard_map/all_gather | solution.py:73
  112.5 2.9 copy-start.3
  115.9 2.4 copy-start.4
  125.9 2.9 copy-start.3
  129.4 2.4 copy-start.4
  139.4 2.9 copy-start.3
  142.9 2.4 copy-start.4
  152.9 2.9 copy-start.3
  156.4 2.4 copy-start.4
  166.3 2.9 copy-start.3
  169.9 2.4 copy-start.4
  179.8 2.9 copy-start.3
  183.3 2.4 copy-start.4
  193.3 2.9 copy-start.3
  196.8 2.4 copy-start.4
  206.8 2.9 copy-start.3
  210.3 2.4 copy-start.4
  220.3 2.9 copy-start.3
  223.8 2.4 copy-start.4
  233.8 2.9 copy-start.3
  237.2 2.4 copy-start.4
  247.2 2.9 copy-start.3
  250.7 2.4 copy-start.4
  260.7 2.9 copy-start.3
  264.2 2.4 copy-start.4
  274.2 2.9 copy-start.3
  277.7 2.4 copy-start.4
  287.7 2.9 copy-start.3
  291.2 2.4 copy-start.4
  305.9 11.4 %copy-start.6 = (s32[16,8,4,2]{0,3,2,1:T(2,128)S(1)}, s32[16,8,4,2]{0,3,2,1:T(2,128)}, u32[]{:S(2)}) copy-start(s32[16,8,4,2]{0,3,2,1:T(2,128)} %param.19) | copy-start | bytes 12292
  305.9 11.7 %copy-start.8 = (f32[2048]{0:T(1024)S(1)}, f32[2048]{0:T(1024)}, u32[]{:S(2)}) copy-start(f32[2048]{0:T(1024)} %param.17) | copy-start | bytes 24580
  305.9 11.7 %copy-start.2 = (s32[64,8,128]{2,1,0:T(8,128)S(1)}, s32[64,8,128]{2,1,0:T(8,128)}, u32[]{:S(2)}) copy-start(s32[64,8,128]{2,1,0:T(8,128)} %fusion.43) | copy-start | bytes 786436
  308.3 28.6 %all-to-all-start = ((bf16[8,256,128]{2,0,1:T(8,128)(2,1)}), bf16[8,256,128]{2,0,1:T(8,128)(2,1)S(1)}, u32[]{:S(2)}, u32[]{:S(2)}) async-start(bf16[8,256,128]{2,0,1:T(8,128)(2,1)} %fusion.38), calls=%async_computation | async-start | bytes 1048576 | tf_op jit(solution)/shard_map/all_to_all | solution.py:90
  422.2 4.5 copy-start.7
  422.2 51.6 %all-to-all-start.2 = ((bf16[4,512,512]{2,0,1:T(4,128)(2,1)}), bf16[4,512,512]{2,0,1:T(4,128)(2,1)S(1)}, u32[]{:S(2)}, u32[]{:S(2)}) async-start(bf16[4,512,512]{2,0,1:T(4,128)(2,1)} %copy.159), calls=%async_computation.2 | async-start | bytes 4194304 | tf_op jit(solution)/shard_map/all_to_all | solution.py:130
  473.8 1.4 copy-start.1
Sparse Core Ops, SparseCore 0:
  9.8 97.2 all-gather.1
where the time goes:
time: 499 us; the launch traced here: 494 us
  waiting for transfers between devices  124 us (25%)
  other arithmetic  110 us (22%)
  local copies, waits for them, and re-layouts  84.8 us (17%)
  matrix products  73.9 us (15%)
  blocking collectives  52.7 us (11%)
  loops' own time  21.3 us (4%)
  between operations  14.4 us (3%)
  starting transfers between devices  13.5 us (3%)
    all_gather x1, waiting for transfers between devices, body(): shard_part = lax.all_gather(stacked, 'seq', axis=2, tiled=True)  94.3 us
    all_to_all x1, blocking collectives, body(): lax.all_to_all(outgoing, 'exp', split_axis=0, concat_axis=1, tiled=True)  52.7 us
    dot_general x14, matrix products, update(): jnp.einsum('bhqk,bkhd->bhqd', rounded_result, shaped[1], preferred_elemen...  34 us
    all_to_all x1, waiting for transfers between devices, body(): lax.all_to_all(results, 'exp', split_axis=1, concat_axis=0, tiled=True)  29.3 us
    dot_general x14, matrix products, update(): jnp.einsum('bqhd,bkhd->bhqk', query_heads, shaped[0], preferred_element_t...  28.9 us
    reduce_or x16, other arithmetic, attend_block(): jnp.any(key_seg[:, -1] >= query_seg[:, 0])  22.3 us
    slice x16, local copies, waits for them, and re-layouts, attend_block(): query_pos[-1]  21.3 us
    reduce_sum x14, other arithmetic, update(): totals = totals * rescale_factor + jnp.sum(weights, axis=-1)  21.2 us
  transfers between devices with their start and end apart: 3, of which 2 were waited for; matrix products, arithmetic and copies ran while one was open for 8% of the time, Pallas kernels for 0%

commit v1 on v0

--- a/solution.py
+++ b/solution.py
@@ -70,7 +70,9 @@
             running, query_heads, block, query_pos, query_seg, seg_ids, key_first, score_scale
         )
 
-    shard_part = lax.all_gather(stacked, "seq", axis=2, tiled=True)
+    shard_part = jnp.concatenate(
+        lax.all_to_all(jnp.stack([stacked] * lax.axis_size("seq")), "seq", 0, 0), axis=2
+    )
     row_count = shard_part.shape[2]
     width = min(row_count, local_len)
     repeats = row_count // width

time: 499 us -> 681 us (1.36)
  waiting for transfers between devices: 124 us -> 291 us
  local copies, waits for them, and re-layouts: 84.8 us -> 105 us
  between operations: 14.4 us -> 1.02 us
  starting transfers between devices: 13.5 us -> 20.4 us
    all_to_all x0 -> x1, waiting for transfers between devices: none -> 260 us  [body(): lax.all_to_all(jnp.stack([stacked] * lax.axis_size('seq')), 'seq', 0, 0)]
    all_gather x1 -> x0, waiting for transfers between devices: 94.3 us -> none  [body(): shard_part = lax.all_gather(stacked, 'seq', axis=2, tiled=True)]
    all_to_all x0 -> x1, local copies, waits for them, and re-layouts: none -> 14 us  [body(): lax.all_to_all(jnp.stack([stacked] * lax.axis_size('seq')), 'seq', 0, 0)]
    all_to_all x0 -> x1, starting transfers between devices: none -> 7.57 us  [body(): lax.all_to_all(jnp.stack([stacked] * lax.axis_size('seq')), 'seq', 0, 0)]
  transfers between devices with their start and end apart: 3 -> 3, of which waited for: 2 -> 2; matrix products, arithmetic and copies ran while one was open for 8% -> 6% of each run, Pallas kernels for 0% -> 0%
where the time goes in v1:
time: 681 us; the launch traced here: 676 us
  waiting for transfers between devices  291 us (43%)
  other arithmetic  109 us (16%)
  local copies, waits for them, and re-layouts  105 us (15%)
  matrix products  74 us (11%)
  blocking collectives  54.2 us (8%)
  loops' own time  21.3 us (3%)
  starting transfers between devices  20.4 us (3%)
    all_to_all x1, waiting for transfers between devices, body(): lax.all_to_all(jnp.stack([stacked] * lax.axis_size('seq')), 'seq', 0, 0)  260 us
    all_to_all x1, blocking collectives, body(): lax.all_to_all(outgoing, 'exp', split_axis=0, concat_axis=1, tiled=True)  54.2 us
    dot_general x14, matrix products, update(): jnp.einsum('bhqk,bkhd->bhqd', rounded_result, shaped[1], preferred_elemen...  34 us
    all_to_all x1, waiting for transfers between devices, body(): lax.all_to_all(results, 'exp', split_axis=1, concat_axis=0, tiled=True)  30.8 us
    dot_general x14, matrix products, update(): jnp.einsum('bqhd,bkhd->bhqk', query_heads, shaped[0], preferred_element_t...  29 us
    reduce_or x16, other arithmetic, attend_block(): jnp.any(key_seg[:, -1] >= query_seg[:, 0])  22.4 us
    reduce_sum x14, other arithmetic, update(): totals = totals * rescale_factor + jnp.sum(weights, axis=-1)  21.2 us
    slice x16, local copies, waits for them, and re-layouts, attend_block(): query_pos[-1]  21.2 us
  transfers between devices with their start and end apart: 3, of which 2 were waited for; matrix products, arithmetic and copies ran while one was open for 6% of the time, Pallas kernels for 0%

profile of v1, /device:TPU:7, one launch (start us, length us, event | category | flops | bytes accessed | tf_op | source)
XLA Modules:
  0.0 675.9 jit_solution(15283057003701386479)
XLA Ops:
  2.0 6.2 stack.11
  8.2 7.6 %all-to-all-start = ((bf16[16,2,8,256,128]{4,3,2,1,0:T(8,128)(2,1)}), bf16[16,2,8,256,128]{4,3,2,1,0:T(8,128)(2,1)}, u32[]{:S(2)}, u32[]{:S(2)}) async-start(bf16[16,2,8,256,128]{4,3,2,1,0:T(8,128)(2,1)} %stack.11), calls=%async_computation | async-start | bytes 33554432 | tf_op jit(solution)/shard_map/all_to_all | solution.py:74
  19.0 260.3 %all-to-all-done = bf16[16,2,8,256,128]{4,3,2,1,0:T(8,128)(2,1)} async-done(((bf16[16,2,8,256,128]{4,3,2,1,0:T(8,128)(2,1)}), bf16[16,2,8,256,128]{4,3,2,1,0:T(8,128)(2,1)}, u32[]{:S(2)}, u32[]{:S(2)}) %all-to-all-start) | async-done | bytes 16777248 | tf_op jit(solution)/shard_map/all_to_all | solution.py:74
  279.3 14.0 %copy.167 = bf16[16,2,8,256,128]{4,3,0,2,1:T(8,128)(2,1)} copy(bf16[16,2,8,256,128]{4,3,2,1,0:T(8,128)(2,1)} %all-to-all-done) | data formatting | bytes 33554432 | tf_op jit(solution)/shard_map/all_to_all | solution.py:74
  294.0 198.1 %while.17 = (s32[]{:T(128)}, f32[8,1,256]{2,0,1:T(8,128)S(1)}, f32[8,1,256]{2,0,1:T(8,128)}, f32[8,1,256,128]{3,2,0,1:T(8,128)S(1)}, s32[256]{0:T(256)}, /*index...) while((s32[]{:T(128)}, f32[8,1,256]{2,0,1:T(8,128)S(1)}, ...), condition=%wide.region_6.7_spmd, body=%wide.region_0.6_spmd.sunk | while | flops 277944608 | bytes 10492413 | solution.py:84
  298.7 8.8 %conditional.2 = ((f32[8,1,256]{2,0,1:T(8,128)S(1)}, f32[8,1,256]{2,0,1:T(8,128)}, f32[8,1,256,128]{3,2,0,1:T(8,128)S(1)})) conditional(s32[]{:T(128)} %convert_element_type.119, (f32[8,1,256]{2,0,1:T(8,128)S(1)}, f32[8,1,256]{2,0,1:T(8,128)}, f32[8,1,256,128]{3,2,0,1:T(8,128)S(1)}) %tuple.52, (s32[]{:T(128)}, s32[256]{0:T(256)S(1)}, s32[256]{0:T(256)}, ...), branch_computations={%region_2.0_spmd, %region_3.5_spmd} | conditional | flops 277944576 | bytes 10474604 | solution.py:42
  299.5 2.1 fusion
  302.2 2.4 fusion.5
  304.7 1.5 fusion.4
  312.2 8.8 %conditional.2 = ((f32[8,1,256]{2,0,1:T(8,128)S(1)}, f32[8,1,256]{2,0,1:T(8,128)}, f32[8,1,256,128]{3,2,0,1:T(8,128)S(1)})) conditional(s32[]{:T(128)} %convert_element_type.119, (f32[8,1,256]{2,0,1:T(8,128)S(1)}, f32[8,1,256]{2,0,1:T(8,128)}, f32[8,1,256,128]{3,2,0,1:T(8,128)S(1)}) %tuple.52, (s32[]{:T(128)}, s32[256]{0:T(256)S(1)}, s32[256]{0:T(256)}, ...), branch_computations={%region_2.0_spmd, %region_3.5_spmd} | conditional | flops 277944576 | bytes 10474604 | solution.py:42
  313.0 2.1 fusion
  315.7 2.4 fusion.5
  325.6 8.8 %conditional.2 = ((f32[8,1,256]{2,0,1:T(8,128)S(1)}, f32[8,1,256]{2,0,1:T(8,128)}, f32[8,1,256,128]{3,2,0,1:T(8,128)S(1)})) conditional(s32[]{:T(128)} %convert_element_type.119, (f32[8,1,256]{2,0,1:T(8,128)S(1)}, f32[8,1,256]{2,0,1:T(8,128)}, f32[8,1,256,128]{3,2,0,1:T(8,128)S(1)}) %tuple.52, (s32[]{:T(128)}, s32[256]{0:T(256)S(1)}, s32[256]{0:T(256)}, ...), branch_computations={%region_2.0_spmd, %region_3.5_spmd} | conditional | flops 277944576 | bytes 10474604 | solution.py:42
  326.5 2.1 fusion
  329.2 2.4 fusion.5
  331.6 1.5 fusion.4
  339.1 8.8 %conditional.2 = ((f32[8,1,256]{2,0,1:T(8,128)S(1)}, f32[8,1,256]{2,0,1:T(8,128)}, f32[8,1,256,128]{3,2,0,1:T(8,128)S(1)})) conditional(s32[]{:T(128)} %convert_element_type.119, (f32[8,1,256]{2,0,1:T(8,128)S(1)}, f32[8,1,256]{2,0,1:T(8,128)}, f32[8,1,256,128]{3,2,0,1:T(8,128)S(1)}) %tuple.52, (s32[]{:T(128)}, s32[256]{0:T(256)S(1)}, s32[256]{0:T(256)}, ...), branch_computations={%region_2.0_spmd, %region_3.5_spmd} | conditional | flops 277944576 | bytes 10474604 | solution.py:42
  340.0 2.1 fusion
  342.6 2.4 fusion.5
  352.6 8.8 %conditional.2 = ((f32[8,1,256]{2,0,1:T(8,128)S(1)}, f32[8,1,256]{2,0,1:T(8,128)}, f32[8,1,256,128]{3,2,0,1:T(8,128)S(1)})) conditional(s32[]{:T(128)} %convert_element_type.119, (f32[8,1,256]{2,0,1:T(8,128)S(1)}, f32[8,1,256]{2,0,1:T(8,128)}, f32[8,1,256,128]{3,2,0,1:T(8,128)S(1)}) %tuple.52, (s32[]{:T(128)}, s32[256]{0:T(256)S(1)}, s32[256]{0:T(256)}, ...), branch_computations={%region_2.0_spmd, %region_3.5_spmd} | conditional | flops 277944576 | bytes 10474604 | solution.py:42
  353.4 2.1 fusion
  356.1 2.4 fusion.5
  366.1 8.8 %conditional.2 = ((f32[8,1,256]{2,0,1:T(8,128)S(1)}, f32[8,1,256]{2,0,1:T(8,128)}, f32[8,1,256,128]{3,2,0,1:T(8,128)S(1)})) conditional(s32[]{:T(128)} %convert_element_type.119, (f32[8,1,256]{2,0,1:T(8,128)S(1)}, f32[8,1,256]{2,0,1:T(8,128)}, f32[8,1,256,128]{3,2,0,1:T(8,128)S(1)}) %tuple.52, (s32[]{:T(128)}, s32[256]{0:T(256)S(1)}, s32[256]{0:T(256)}, ...), branch_computations={%region_2.0_spmd, %region_3.5_spmd} | conditional | flops 277944576 | bytes 10474604 | solution.py:42
  366.9 2.1 fusion
  369.6 2.4 fusion.5
  379.5 8.8 %conditional.2 = ((f32[8,1,256]{2,0,1:T(8,128)S(1)}, f32[8,1,256]{2,0,1:T(8,128)}, f32[8,1,256,128]{3,2,0,1:T(8,128)S(1)})) conditional(s32[]{:T(128)} %convert_element_type.119, (f32[8,1,256]{2,0,1:T(8,128)S(1)}, f32[8,1,256]{2,0,1:T(8,128)}, f32[8,1,256,128]{3,2,0,1:T(8,128)S(1)}) %tuple.52, (s32[]{:T(128)}, s32[256]{0:T(256)S(1)}, s32[256]{0:T(256)}, ...), branch_computations={%region_2.0_spmd, %region_3.5_spmd} | conditional | flops 277944576 | bytes 10474604 | solution.py:42
  380.4 2.1 fusion
  383.1 2.4 fusion.5
  393.0 8.8 %conditional.2 = ((f32[8,1,256]{2,0,1:T(8,128)S(1)}, f32[8,1,256]{2,0,1:T(8,128)}, f32[8,1,256,128]{3,2,0,1:T(8,128)S(1)})) conditional(s32[]{:T(128)} %convert_element_type.119, (f32[8,1,256]{2,0,1:T(8,128)S(1)}, f32[8,1,256]{2,0,1:T(8,128)}, f32[8,1,256,128]{3,2,0,1:T(8,128)S(1)}) %tuple.52, (s32[]{:T(128)}, s32[256]{0:T(256)S(1)}, s32[256]{0:T(256)}, ...), branch_computations={%region_2.0_spmd, %region_3.5_spmd} | conditional | flops 277944576 | bytes 10474604 | solution.py:42
  393.8 2.1 fusion
  396.5 2.4 fusion.5
  406.5 8.8 %conditional.2 = ((f32[8,1,256]{2,0,1:T(8,128)S(1)}, f32[8,1,256]{2,0,1:T(8,128)}, f32[8,1,256,128]{3,2,0,1:T(8,128)S(1)})) conditional(s32[]{:T(128)} %convert_element_type.119, (f32[8,1,256]{2,0,1:T(8,128)S(1)}, f32[8,1,256]{2,0,1:T(8,128)}, f32[8,1,256,128]{3,2,0,1:T(8,128)S(1)}) %tuple.52, (s32[]{:T(128)}, s32[256]{0:T(256)S(1)}, s32[256]{0:T(256)}, ...), branch_computations={%region_2.0_spmd, %region_3.5_spmd} | conditional | flops 277944576 | bytes 10474604 | solution.py:42
  407.3 2.1 fusion
  410.0 2.4 fusion.5
  420.0 8.8 %conditional.2 = ((f32[8,1,256]{2,0,1:T(8,128)S(1)}, f32[8,1,256]{2,0,1:T(8,128)}, f32[8,1,256,128]{3,2,0,1:T(8,128)S(1)})) conditional(s32[]{:T(128)} %convert_element_type.119, (f32[8,1,256]{2,0,1:T(8,128)S(1)}, f32[8,1,256]{2,0,1:T(8,128)}, f32[8,1,256,128]{3,2,0,1:T(8,128)S(1)}) %tuple.52, (s32[]{:T(128)}, s32[256]{0:T(256)S(1)}, s32[256]{0:T(256)}, ...), branch_computations={%region_2.0_spmd, %region_3.5_spmd} | conditional | flops 277944576 | bytes 10474604 | solution.py:42
  420.8 2.1 fusion
  423.5 2.4 fusion.5
  433.4 8.8 %conditional.2 = ((f32[8,1,256]{2,0,1:T(8,128)S(1)}, f32[8,1,256]{2,0,1:T(8,128)}, f32[8,1,256,128]{3,2,0,1:T(8,128)S(1)})) conditional(s32[]{:T(128)} %convert_element_type.119, (f32[8,1,256]{2,0,1:T(8,128)S(1)}, f32[8,1,256]{2,0,1:T(8,128)}, f32[8,1,256,128]{3,2,0,1:T(8,128)S(1)}) %tuple.52, (s32[]{:T(128)}, s32[256]{0:T(256)S(1)}, s32[256]{0:T(256)}, ...), branch_computations={%region_2.0_spmd, %region_3.5_spmd} | conditional | flops 277944576 | bytes 10474604 | solution.py:42
  434.3 2.1 fusion
  437.0 2.4 fusion.5
  446.9 8.8 %conditional.2 = ((f32[8,1,256]{2,0,1:T(8,128)S(1)}, f32[8,1,256]{2,0,1:T(8,128)}, f32[8,1,256,128]{3,2,0,1:T(8,128)S(1)})) conditional(s32[]{:T(128)} %convert_element_type.119, (f32[8,1,256]{2,0,1:T(8,128)S(1)}, f32[8,1,256]{2,0,1:T(8,128)}, f32[8,1,256,128]{3,2,0,1:T(8,128)S(1)}) %tuple.52, (s32[]{:T(128)}, s32[256]{0:T(256)S(1)}, s32[256]{0:T(256)}, ...), branch_computations={%region_2.0_spmd, %region_3.5_spmd} | conditional | flops 277944576 | bytes 10474604 | solution.py:42
  447.8 2.1 fusion
  450.4 2.4 fusion.5
  460.4 8.8 %conditional.2 = ((f32[8,1,256]{2,0,1:T(8,128)S(1)}, f32[8,1,256]{2,0,1:T(8,128)}, f32[8,1,256,128]{3,2,0,1:T(8,128)S(1)})) conditional(s32[]{:T(128)} %convert_element_type.119, (f32[8,1,256]{2,0,1:T(8,128)S(1)}, f32[8,1,256]{2,0,1:T(8,128)}, f32[8,1,256,128]{3,2,0,1:T(8,128)S(1)}) %tuple.52, (s32[]{:T(128)}, s32[256]{0:T(256)S(1)}, s32[256]{0:T(256)}, ...), branch_computations={%region_2.0_spmd, %region_3.5_spmd} | conditional | flops 277944576 | bytes 10474604 | solution.py:42
  461.2 2.1 fusion
  463.9 2.4 fusion.5
  473.9 8.8 %conditional.2 = ((f32[8,1,256]{2,0,1:T(8,128)S(1)}, f32[8,1,256]{2,0,1:T(8,128)}, f32[8,1,256,128]{3,2,0,1:T(8,128)S(1)})) conditional(s32[]{:T(128)} %convert_element_type.119, (f32[8,1,256]{2,0,1:T(8,128)S(1)}, f32[8,1,256]{2,0,1:T(8,128)}, f32[8,1,256,128]{3,2,0,1:T(8,128)S(1)}) %tuple.52, (s32[]{:T(128)}, s32[256]{0:T(256)S(1)}, s32[256]{0:T(256)}, ...), branch_computations={%region_2.0_spmd, %region_3.5_spmd} | conditional | flops 277944576 | bytes 10474604 | solution.py:42
  474.7 2.1 fusion
  477.4 2.4 fusion.5
  494.5 8.4 %all-to-all-start.1 = ((bf16[8,256,128]{2,0,1:T(8,128)(2,1)}), bf16[8,256,128]{2,0,1:T(8,128)(2,1)S(1)}, u32[]{:S(2)}, u32[]{:S(2)}) async-start(bf16[8,256,128]{2,0,1:T(8,128)(2,1)} %fusion.38), calls=%async_computation.1 | async-start | bytes 1048576 | tf_op jit(solution)/shard_map/all_to_all | solution.py:92
  503.2 18.0 %reduce-window.6 = s32[64,8,128]{2,1,0:T(8,128)S(1)} reduce-window(s32[64,8,128]{2,1,0:T(8,128)S(1)} %copy-done.3, s32[]{:T(128)} %constant.101.clone.1), window={size=1x1x128 pad=0_0x0_0x127_0}, to_apply=%region_10.11 | reduce-window | flops 8323072 | bytes 524292 | tf_op jit(solution)/shard_map/reduce-window
  522.6 1.6 copy.173
  524.2 1.6 reshape.321
  527.4 13.1 %scatter_custom_fusion = bf16[2048,512]{1,0:T(8,128)(2,1)S(1)} fusion(s32[1024]{0:T(1024)S(1)} %bitcast.126, bf16[512,512]{1,0:T(8,128)(2,1)} %reshape.315, s32[1024]{0:T(1024)S(1)} %broadcast_clamp_fusion.1, bf16[]{:T(256)} %constant.114.clone.1), kind=kCustom, calls=%fused_computation.52 | custom fusion | bytes 2097664 | tf_op jit(solution)/shard_map/scatter | solution.py:121
  540.5 54.2 %all_to_all.47 = bf16[64,32,512]{2,1,0:T(8,128)(2,1)S(1)} all-to-all(bf16[64,32,512]{2,1,0:T(8,128)(2,1)S(1)} %bitcast.114), channel_id=1, replica_groups=mesh['seq'=16,'exp'=16] {'exp'}, dimensions={0} | all-to-all | bytes 4194304 | tf_op jit(solution)/shard_map/all_to_all | solution.py:124
  594.9 9.7 %fusion.31 = bf16[4,512,512]{2,1,0:T(8,128)(2,1)} fusion(bf16[4,1024,512]{2,1,0:T(8,128)(2,1)} %param.21, bf16[4,512,512]{2,1,0:T(8,128)(2,1)S(1)} %bitcast.118, bf16[4,512,1024]{2,1,0:T(8,128)(2,1)} %param.20), kind=kOutput, calls=%fused_computation.48 | convolution fusion | flops 4314890240 | bytes 12582912 | tf_op jit(solution)/shard_map/ecf,efs->ecs/dot_general | solution.py:129
  604.7 4.6 copy.189
  609.2 4.5 all-to-all-start.3
  615.9 8.6 %gather_fusion.1 = f32[1024]{0:T(1024)S(1)} fusion(f32[512,64]{0,1:T(8,128)S(1)} %fusion.54, s32[1024]{0:T(1024)S(1)} %reshape.341), kind=kCustom, calls=%fused_computation.2 | custom fusion | bytes 16384 | tf_op jit(solution)/shard_map/jit(take_along_axis)/gather | solution.py:106
  625.7 1.6 copy.170
  631.6 30.8 %all-to-all-done.3 = bf16[4,512,512]{2,0,1:T(4,128)(2,1)S(1)} async-done(((bf16[4,512,512]{2,0,1:T(4,128)(2,1)}), bf16[4,512,512]{2,0,1:T(4,128)(2,1)S(1)}, u32[]{:S(2)}, u32[]{:S(2)}) %all-to-all-start.3) | async-done | bytes 2097184 | tf_op jit(solution)/shard_map/all_to_all | solution.py:132
  663.7 2.2 copy.190
  665.9 4.0 gather_fusion
  671.2 3.2 multiply_reduce_fusion
  (277 shorter events, 133.4 us)
Async XLA Ops:
  0.6 613.9 %copy-start = (bf16[512,64]{0,1:T(8,128)(2,1)S(1)}, bf16[512,64]{0,1:T(8,128)(2,1)}, u32[]{:S(2)}) copy-start(bf16[512,64]{0,1:T(8,128)(2,1)} %param.18) | copy-start | bytes 196612
  8.2 7.6 %copy-start.6 = (s32[16,8,4,2]{0,3,2,1:T(2,128)S(1)}, s32[16,8,4,2]{0,3,2,1:T(2,128)}, u32[]{:S(2)}) copy-start(s32[16,8,4,2]{0,3,2,1:T(2,128)} %param.19) | copy-start | bytes 12292
  8.2 271.1 %all-to-all-start = ((bf16[16,2,8,256,128]{4,3,2,1,0:T(8,128)(2,1)}), bf16[16,2,8,256,128]{4,3,2,1,0:T(8,128)(2,1)}, u32[]{:S(2)}, u32[]{:S(2)}) async-start(bf16[16,2,8,256,128]{4,3,2,1,0:T(8,128)(2,1)} %stack.11), calls=%async_computation | async-start | bytes 33554432 | tf_op jit(solution)/shard_map/all_to_all | solution.py:74
  298.7 2.9 copy-start.4
  302.2 2.4 copy-start.5
  312.2 2.9 copy-start.4
  315.7 2.4 copy-start.5
  325.7 2.9 copy-start.4
  329.2 2.4 copy-start.5
  339.2 2.9 copy-start.4
  342.6 2.4 copy-start.5
  352.6 2.9 copy-start.4
  356.1 2.4 copy-start.5
  366.1 2.9 copy-start.4
  369.6 2.4 copy-start.5
  379.6 2.9 copy-start.4
  383.1 2.4 copy-start.5
  393.0 2.9 copy-start.4
  396.5 2.4 copy-start.5
  406.5 2.9 copy-start.4
  410.0 2.4 copy-start.5
  420.0 2.9 copy-start.4
  423.5 2.4 copy-start.5
  433.5 2.9 copy-start.4
  437.0 2.4 copy-start.5
  447.0 2.9 copy-start.4
  450.4 2.4 copy-start.5
  460.4 2.9 copy-start.4
  463.9 2.4 copy-start.5
  473.9 2.9 copy-start.4
  477.4 2.4 copy-start.5
  492.1 10.8 %copy-start.7 = (s32[16,8,4,2]{0,3,2,1:T(2,128)S(1)}, s32[16,8,4,2]{0,3,2,1:T(2,128)}, u32[]{:S(2)}) copy-start(s32[16,8,4,2]{0,3,2,1:T(2,128)} %param.19) | copy-start | bytes 12292
  492.1 11.1 %copy-start.9 = (f32[2048]{0:T(1024)S(1)}, f32[2048]{0:T(1024)}, u32[]{:S(2)}) copy-start(f32[2048]{0:T(1024)} %param.17) | copy-start | bytes 24580
  492.1 11.1 %copy-start.3 = (s32[64,8,128]{2,1,0:T(8,128)S(1)}, s32[64,8,128]{2,1,0:T(8,128)}, u32[]{:S(2)}) copy-start(s32[64,8,128]{2,1,0:T(8,128)} %fusion.43) | copy-start | bytes 786436
  494.5 28.0 %all-to-all-start.1 = ((bf16[8,256,128]{2,0,1:T(8,128)(2,1)}), bf16[8,256,128]{2,0,1:T(8,128)(2,1)S(1)}, u32[]{:S(2)}, u32[]{:S(2)}) async-start(bf16[8,256,128]{2,0,1:T(8,128)(2,1)} %fusion.38), calls=%async_computation.1 | async-start | bytes 1048576 | tf_op jit(solution)/shard_map/all_to_all | solution.py:92
  609.2 4.5 copy-start.8
  609.2 53.1 %all-to-all-start.3 = ((bf16[4,512,512]{2,0,1:T(4,128)(2,1)}), bf16[4,512,512]{2,0,1:T(4,128)(2,1)S(1)}, u32[]{:S(2)}, u32[]{:S(2)}) async-start(bf16[4,512,512]{2,0,1:T(4,128)(2,1)} %copy.189), calls=%async_computation.3 | async-start | bytes 4194304 | tf_op jit(solution)/shard_map/all_to_all | solution.py:132
  662.4 1.4 copy-start.2
  669.8 6.0 copy-start.1
